TPU v7x, 32 devices: a whole 2x2x4 slice. The times are simulated.
32 devices in a mesh: dp: 8 (over z, y), mp: 4 (over x, core).
Axes of the slice: x: 2, y: 2, z: 4, core: 2. Of those that a mesh axis runs over, the one named last changes fastest.
Arguments:
- tokens: bfloat16 [12288, 768], P('dp'), may hold values from -6 to 6
- segment_ids: int32 [12288], P('dp'), may hold values from 0 to 47, as said below
- first_gain: bfloat16 [768], replicated, may hold values from 0.25 to 1.75
- first_shift: bfloat16 [768], replicated, may hold values from -3 to 3
- qkv_weight: bfloat16 [768, 3, 768], P(None, None, 'mp'), may hold values from -0.21875 to 0.21875
- qv_bias: bfloat16 [2, 12, 64], P(None, 'mp'), may hold values from -3 to 3
- proj_weight: bfloat16 [768, 768], P('mp'), may hold values from -1.25 to 1.25
- proj_bias: bfloat16 [768], replicated, may hold values from -3 to 3
- second_gain: bfloat16 [768], replicated, may hold values from 0.25 to 1.75
- second_shift: bfloat16 [768], replicated, may hold values from -3 to 3
- up_weight: bfloat16 [768, 3072], P(None, 'mp'), may hold values from -0.21875 to 0.21875
- up_bias: bfloat16 [48, 64], P('mp'), may hold values from -3 to 3
- down_weight: bfloat16 [3072, 768], P('mp'), may hold values from -0.109375 to 0.109375
- down_bias: bfloat16 [768], replicated, may hold values from -3 to 3
- cotangent: bfloat16 [12288, 768], P('dp'), may hold values from -6 to 6
Outputs:
- layer_output: bfloat16 [12288, 768], P('dp')
- input_grad: bfloat16 [12288, 768], P('dp')
- first_gain_grad: float32 [768], P('dp')
- first_shift_grad: float32 [768], P('dp')
- qkv_weight_grad: float32 [768, 3, 768], P('dp', None, 'mp')
- qv_bias_grad: float32 [2, 12, 64], P(None, 'mp', 'dp')
- proj_weight_grad: float32 [768, 768], P('mp', 'dp')
- proj_bias_grad: float32 [768], P('dp')
- second_gain_grad: float32 [768], P('dp')
- second_shift_grad: float32 [768], P('dp')
- up_weight_grad: float32 [768, 3072], P('dp', 'mp')
- up_bias_grad: float32 [48, 64], P('mp', 'dp')
- down_weight_grad: float32 [3072, 768], P('mp', 'dp')
- down_bias_grad: float32 [768], P('dp')
Inputs may be any that keep to these rules, and one draw needn't show every extreme that they name: `segment_ids`: in each sequence of 512 tokens the first 16 * r tokens carry one even id and the others that id plus one, with r from 8 to 24; different sequences have different ids.
All inputs are finite; a program needn't handle non-finite values.
Results may differ from a plain program's by a relative error of at most 0.013.
Values sent between devices are 32-bit elements; how exact they have to be, the bound alone decides.
A program may use at most 128 MiB of HBM per device.

v0:
```python
import jax
import jax.numpy as jnp
from jax import lax
from jax.sharding import PartitionSpec as P

LEN = 512
EPS = 1e-06
SCALE = 0.125
NEGATIVE = -1e30


def normalize(values):
    centre = values - jnp.mean(values, axis=-1, keepdims=True)
    inverse = lax.rsqrt(jnp.mean(centre * centre, axis=-1, keepdims=True) + EPS)
    return (centre * inverse, inverse)


def norm_backward(grad_normed, unit, inverse, gain):
    scaled = grad_normed * gain
    return inverse * (
        scaled
        - jnp.mean(scaled, axis=-1, keepdims=True)
        - unit * jnp.mean(scaled * unit, axis=-1, keepdims=True)
    )


def exact_gelu(values):
    return jax.nn.gelu(values, approximate=False)


def masked_scores(query, keys, labels):
    raw = jnp.einsum("qhe,khe->hqk", query, keys, preferred_element_type=jnp.float32)
    same = labels[:, None] == labels[None, :]
    return jnp.where(same[None], SCALE * raw, NEGATIVE)


def attend(items):
    triple, labels = items
    scores = masked_scores(triple[:, 0], triple[:, 1], labels)
    top = jnp.max(scores, axis=-1, keepdims=True)
    expo = jnp.exp(scores - top)
    total = jnp.sum(expo, axis=-1, keepdims=True)
    probs = expo / total
    mixed = jnp.einsum(
        "hqk,khe->qhe", probs.astype(jnp.bfloat16), triple[:, 2], preferred_element_type=jnp.float32
    )
    return (mixed.astype(jnp.bfloat16), top + jnp.log(total))


def attend_back(items):
    triple, labels, grad_mixed, log_total = items
    query = triple[:, 0]
    keys = triple[:, 1]
    values = triple[:, 2]
    probs = jnp.exp(masked_scores(query, keys, labels) - log_total)
    grad_probs = jnp.einsum("qhe,khe->hqk", grad_mixed, values, preferred_element_type=jnp.float32)
    inner = jnp.sum(probs * grad_probs, axis=-1, keepdims=True)
    grad_scores = (probs * (grad_probs - inner)).astype(jnp.bfloat16)
    grad_query = SCALE * jnp.einsum(
        "hqk,khe->qhe", grad_scores, keys, preferred_element_type=jnp.float32
    )
    grad_keys = SCALE * jnp.einsum(
        "hqk,qhe->khe", grad_scores, query, preferred_element_type=jnp.float32
    )
    grad_values = jnp.einsum(
        "hqk,qhe->khe", probs.astype(jnp.bfloat16), grad_mixed, preferred_element_type=jnp.float32
    )
    return jnp.stack([grad_query, grad_keys, grad_values], axis=1).astype(jnp.bfloat16)


def shards(
    tokens,
    segment_ids,
    first_gain,
    first_shift,
    qkv_weight,
    qv_bias,
    proj_weight,
    proj_bias,
    second_gain,
    second_shift,
    up_weight,
    up_bias,
    down_weight,
    down_bias,
    cotangent,
):
    rows = tokens.shape[0]
    heads_here = qv_bias.shape[1]
    head_size = qv_bias.shape[2]
    local_width = heads_here * head_size
    count = rows // LEN
    gain_one = first_gain.astype(jnp.float32)
    gain_two = second_gain.astype(jnp.float32)
    inputs = tokens.astype(jnp.float32)
    first_unit, first_inverse = normalize(inputs)
    normed1 = (first_unit * gain_one + first_shift.astype(jnp.float32)).astype(jnp.bfloat16)
    projected = jnp.einsum("nd,dce->nce", normed1, qkv_weight, preferred_element_type=jnp.float32)
    query_bias = qv_bias[0].reshape(local_width).astype(jnp.float32)
    bias_rows = jnp.stack(
        [
            query_bias,
            jnp.zeros_like(query_bias),
            qv_bias[1].reshape(local_width).astype(jnp.float32),
        ]
    )
    triple = (
        (projected + bias_rows).astype(jnp.bfloat16).reshape(count, LEN, 3, heads_here, head_size)
    )
    image_ids = segment_ids.reshape(count, LEN)
    mixed, log_total = lax.map(attend, (triple, image_ids))
    mixed_rows = mixed.reshape(rows, local_width)
    head_part = jnp.dot(mixed_rows, proj_weight, preferred_element_type=jnp.float32)
    attended = lax.psum(head_part, "mp")
    middle = inputs + attended + proj_bias.astype(jnp.float32)
    second_unit, second_inverse = normalize(middle)
    normed2 = (second_unit * gain_two + second_shift.astype(jnp.float32)).astype(jnp.bfloat16)
    up_flat = up_bias.reshape(-1).astype(jnp.float32)
    hidden_pre = jnp.dot(normed2, up_weight, preferred_element_type=jnp.float32) + up_flat
    activated, gelu_pull = jax.vjp(exact_gelu, hidden_pre)
    hidden = activated.astype(jnp.bfloat16)
    column_part = jnp.dot(hidden, down_weight, preferred_element_type=jnp.float32)
    fed = lax.psum(column_part, "mp")
    layer_output = (middle + fed + down_bias.astype(jnp.float32)).astype(jnp.bfloat16)
    grad_out = cotangent.astype(jnp.float32)
    down_bias_grad = jnp.sum(grad_out, axis=0)
    down_weight_grad = jnp.einsum(
        "nf,nd->fd", hidden, cotangent, preferred_element_type=jnp.float32
    )
    grad_hidden = jnp.einsum(
        "nd,fd->nf", cotangent, down_weight, preferred_element_type=jnp.float32
    )
    normed_again = lax.optimization_barrier(normed2)
    pre_again = jnp.dot(normed_again, up_weight, preferred_element_type=jnp.float32) + up_flat
    unused, pull_again = jax.vjp(exact_gelu, pre_again)
    grad_pre = pull_again(grad_hidden)[0]
    grad_pre_low = grad_pre.astype(jnp.bfloat16)
    up_bias_grad = jnp.sum(grad_pre_low, axis=0, dtype=jnp.float32).reshape(up_bias.shape)
    up_weight_grad = jnp.einsum(
        "nd,nf->df", normed2, grad_pre_low, preferred_element_type=jnp.float32
    )
    column_back_part = jnp.einsum(
        "nf,df->nd", grad_pre_low, up_weight, preferred_element_type=jnp.float32
    )
    grad_normed2 = lax.psum(column_back_part, "mp")
    second_gain_grad = jnp.sum(grad_normed2 * second_unit, axis=0)
    second_shift_grad = jnp.sum(grad_normed2, axis=0)
    grad_middle = grad_out + norm_backward(grad_normed2, second_unit, second_inverse, gain_two)
    proj_bias_grad = jnp.sum(grad_middle, axis=0)
    middle_low = grad_middle.astype(jnp.bfloat16)
    proj_weight_grad = jnp.einsum(
        "ne,nd->ed", mixed_rows, middle_low, preferred_element_type=jnp.float32
    )
    grad_mixed = jnp.einsum(
        "nd,ed->ne", middle_low, proj_weight, preferred_element_type=jnp.float32
    )
    grad_mixed = grad_mixed.astype(jnp.bfloat16).reshape(count, LEN, heads_here, head_size)
    grad_triple = lax.map(attend_back, (triple, image_ids, grad_mixed, log_total))
    grad_rows = grad_triple.reshape(rows, 3, local_width)
    qv_bias_grad = jnp.stack(
        [
            jnp.sum(grad_rows[:, 0], axis=0, dtype=jnp.float32),
            jnp.sum(grad_rows[:, 2], axis=0, dtype=jnp.float32),
        ]
    ).reshape(2, heads_here, head_size)
    qkv_weight_grad = jnp.einsum(
        "nd,nce->dce", normed1, grad_rows, preferred_element_type=jnp.float32
    )
    head_back_part = jnp.einsum(
        "nce,dce->nd", grad_rows, qkv_weight, preferred_element_type=jnp.float32
    )
    grad_normed1 = lax.psum(head_back_part, "mp")
    first_gain_grad = jnp.sum(grad_normed1 * first_unit, axis=0)
    first_shift_grad = jnp.sum(grad_normed1, axis=0)
    input_grad = (
        grad_middle + norm_backward(grad_normed1, first_unit, first_inverse, gain_one)
    ).astype(jnp.bfloat16)
    summed = (
        lax.psum_scatter(qkv_weight_grad, "dp", scatter_dimension=0, tiled=True),
        lax.psum_scatter(qv_bias_grad, "dp", scatter_dimension=2, tiled=True),
        lax.psum_scatter(proj_weight_grad, "dp", scatter_dimension=1, tiled=True),
        lax.psum_scatter(proj_bias_grad, "dp", scatter_dimension=0, tiled=True),
        lax.psum_scatter(first_gain_grad, "dp", scatter_dimension=0, tiled=True),
        lax.psum_scatter(first_shift_grad, "dp", scatter_dimension=0, tiled=True),
        lax.psum_scatter(down_weight_grad, "dp", scatter_dimension=1, tiled=True),
        lax.psum_scatter(down_bias_grad, "dp", scatter_dimension=0, tiled=True),
        lax.psum_scatter(up_weight_grad, "dp", scatter_dimension=0, tiled=True),
        lax.psum_scatter(up_bias_grad, "dp", scatter_dimension=1, tiled=True),
        lax.psum_scatter(second_gain_grad, "dp", scatter_dimension=0, tiled=True),
        lax.psum_scatter(second_shift_grad, "dp", scatter_dimension=0, tiled=True),
    )
    head_sums = summed[:6]
    column_sums = summed[6:]
    return (
        layer_output,
        input_grad,
        head_sums[4],
        head_sums[5],
        head_sums[0],
        head_sums[1],
        head_sums[2],
        head_sums[3],
        column_sums[4],
        column_sums[5],
        column_sums[2],
        column_sums[3],
        column_sums[0],
        column_sums[1],
    )


def solution(mesh):
    in_specs = (
        P("dp", None),
        P("dp"),
        P(),
        P(),
        P(None, None, "mp"),
        P(None, "mp", None),
        P("mp", None),
        P(),
        P(),
        P(),
        P(None, "mp"),
        P("mp", None),
        P("mp", None),
        P(),
        P("dp", None),
    )
    out_specs = (
        P("dp", None),
        P("dp", None),
        P("dp"),
        P("dp"),
        P("dp", None, "mp"),
        P(None, "mp", "dp"),
        P("mp", "dp"),
        P("dp"),
        P("dp"),
        P("dp"),
        P("dp", "mp"),
        P("mp", "dp"),
        P("mp", "dp"),
        P("dp"),
    )
    return jax.shard_map(shards, mesh=mesh, in_specs=in_specs, out_specs=out_specs, check_vma=False)
```

profile of v0, /device:TPU:0, one launch (start us, length us, event | category | flops | bytes accessed | tf_op | source)
XLA Modules:
  0.0 749.1 jit_solution(18400123247982179600)
XLA Ops:
  7.3 0.8 convert_element_type.122
  11.6 2.1 convert_reduce_fusion
  13.8 2.5 fusion.42
  16.5 1.8 fusion.71
  18.3 1.5 add_convert_fusion.2
  19.8 5.2 reshape.266
  24.9 3.4 copy.53
  28.3 15.6 %while.22 = (s32[]{:T(128)}, bf16[3,512,3,64]{1,3,2,0:T(8,128)(2,1)}, f32[3,3,512,1]{2,1,3,0:T(4,128)}, bf16[3,512,3,3,64]{1,4,3,2,0:T(8,128)(2,1)}, s32[3,512]{1,0:T(4,128)S(1)}, /*index=5*/s32[]{:T(128)}) while((s32[]{:T(128)}, bf16[3,512,3,64]{1,3,2,0:T(8,128)(2,1)}, f32[3,3,512,1]{2,1,3,0:T(4,128)}, bf16[3,512,3,3,64]{1,4,3,2,0:T(8,128)(2,1)}, ...), condition=%wide.region_5.6_spmd, body=%wide.region_2.5_spmd.sunk | while | flops 211122688 | bytes 12513373 | solution.py:111
  28.5 1.1 dynamic-slice_bitcast_fusion.6
  31.1 1.7 fusion.120
  33.7 1.1 dynamic-slice_bitcast_fusion.6
  36.3 1.8 fusion.120
  38.9 1.1 dynamic-slice_bitcast_fusion.6
  41.5 1.8 fusion.120
  43.9 1.6 copy.54
  46.5 4.0 fusion.76
  52.4 1.3 convert_element_type.132
  53.7 6.4 fusion.78
  60.1 87.3 %all-reduce.14.cloned.1.call-done = f32[1536,768]{1,0:T(8,128)} async-done(((f32[1536,768]{1,0:T(8,128)}), f32[1536,768]{1,0:T(8,128)}) %all-reduce.14.cloned.1.call-update) | async-done | bytes 4718608 | tf_op jit(solution)/shard_map/psum | solution.py:114
  147.4 3.1 fusion.74
  151.3 1.1 add_convert_fusion.1
  152.9 1.5 slice-done.3
  154.4 14.3 %convert_reduce_fusion.2 = (f32[768]{0:T(1024)}, bf16[1536,768]{1,0:T(8,128)(2,1)S(1)}) fusion(f32[1536,768]{1,0:T(8,128)S(1)} %bitcast.167, f32[768]{0:T(1024)S(1)} %copy-done.37, bf16[1536,768]{1,0:T(8,128)(2,1)S(1)} %add_convert_fusion.1, bf16[768,768]{1,0:T(8,128)(2,1)S(1)} %copy-done), kind=kOutput, calls=%fused_computation.78 | convolution fusion | flops 1900412160 | bytes 10622976 | tf_op jit(solution)/shard_map/dot_general | solution.py:134
  168.7 1.4 copy-done.12
  170.1 4.2 fusion.79
  175.0 12.9 %fusion.46 = bf16[1536,768]{1,0:T(8,128)(2,1)S(1)} fusion(bf16[1536,768]{1,0:T(8,128)(2,1)S(1)} %add_convert_fusion.1, bf16[768,768]{1,0:T(8,128)(2,1)S(1)} %copy-done, f32[768]{0:T(1024)} %reshape.274), kind=kOutput, calls=%fused_computation.72 | convolution fusion | flops 1889796096 | bytes 5901312 | tf_op jit(solution)/shard_map/dot_general | solution.py:119
  187.9 1.5 copy-done.47
  189.4 4.3 fusion.77
  193.7 75.0 %all-reduce.16.cloned.1.call-done = f32[1536,768]{1,0:T(8,128)} async-done(((f32[1536,768]{1,0:T(8,128)}), f32[1536,768]{1,0:T(8,128)}) %all-reduce.16.cloned.1.call-update) | async-done | bytes 4718608 | tf_op jit(solution)/shard_map/psum | solution.py:145
  268.7 5.6 multiply_reduce_fusion.1
  274.3 4.9 fusion.73
  279.3 2.2 copy-done.3
  281.4 1.9 convolution_bitcast_fusion.1
  283.4 3.4 convolution_convert_fusion
  287.6 21.1 %while.23 = (s32[]{:T(128)}, bf16[3,512,3,3,64]{1,4,3,2,0:T(8,128)(2,1)S(1)}, bf16[3,512,3,3,64]{1,4,3,2,0:T(8,128)(2,1)}, s32[3,512]{1,0:T(4,128)}, f32[3,3,512...) while((s32[]{:T(128)}, bf16[3,512,3,3,64]{1,4,3,2,0:T(8,128)(2,1)S(1)}, ...), condition=%wide.region_15.16_spmd, body=%wide.region_13.15_spmd.sunk | while | flops 512915968 | bytes 28481644 | solution.py:158
  289.3 1.1 dynamic-slice_bitcast_fusion.7
  291.0 1.1 multiply_reduce_fusion.7
  292.1 0.8 multiply_convert_fusion.2
  296.3 1.1 dynamic-slice_bitcast_fusion.7
  298.0 1.2 multiply_reduce_fusion.7
  299.2 0.8 multiply_convert_fusion.2
  303.3 1.1 dynamic-slice_bitcast_fusion.7
  305.1 1.1 multiply_reduce_fusion.7
  306.2 0.8 multiply_convert_fusion.2
  308.7 1.2 copy-done.16
  309.9 3.1 copy.57
  313.0 3.8 reshape.270
  316.8 5.8 convolution_bitcast_fusion
  322.6 1.6 copy-done.14
  324.2 5.1 fusion.81
  329.7 6.1 fusion.80
  336.0 5.4 fusion.66
  343.5 1.5 convert_reduce_fusion.4
  345.1 5.3 reduce-scatter.15.cloned.1.call-done
  350.5 1.6 copy.70
  352.1 169.7 %all-reduce.18.cloned.1.call-done = (f32[1536,768]{1,0:T(8,128)}, f32[1536,768]{1,0:T(8,128)}) async-done(((f32[1536,768]{1,0:T(8,128)}, f32[1536,768]{1,0:T(8,128)}), (f32[1536,768]{1,0:T(8,128)}, f32[1536,768]{1,0:T(8,128)})) %all-reduce.18.cloned.1.call-update) | async-done | bytes 9437200 | tf_op jit(solution)/shard_map/psum | solution.py:123
  521.8 4.3 fusion.41
  526.2 37.9 %all-reduce.8 = (f32[768]{0:T(1024)S(1)}, f32[768]{0:T(1024)S(1)}, f32[2,3,64]{2,1,0:T(4,128)S(1)}, f32[768]{0:T(1024)S(1)}, f32[768]{0:T(1024)S(1)}, /*index=5*...) all-reduce(f32[768]{0:T(1024)S(1)} %get-tuple-element.140, ...), channel_id=2, replica_groups=mesh['dp'=8,'mp'=4] {'dp'}, use_global_device_ids=true, to_apply=%region_20.21.clone | all-reduce | flops 5760 | bytes 46080
  569.0 6.0 add_convert_fusion
  575.0 1.9 copy-done.8
  576.9 2.8 fusion.40
  579.8 16.4 %reduce-scatter.13.cloned.1.call-done = f32[768,96]{0,1:T(8,128)} async-done(((f32[768,768]{0,1:T(8,128)}), f32[768,96]{0,1:T(8,128)}) %reduce-scatter.13.cloned.1.call-update) | async-done | bytes 294928 | tf_op jit(solution)/shard_map/reduce_scatter | solution.py:185
  596.2 72.9 %reduce-scatter.11.cloned.1.call-done = f32[96,768]{1,0:T(8,128)} async-done(((f32[768,768]{1,0:T(8,128)}), f32[96,768]{1,0:T(8,128)}) %reduce-scatter.11.cloned.1.call-update) | async-done | bytes 294928 | tf_op jit(solution)/shard_map/reduce_scatter | solution.py:187
  669.0 72.9 %reduce-scatter.9.cloned.1.call-done = f32[96,3,192]{2,0,1:T(8,128)} async-done(((f32[768,3,192]{2,0,1:T(8,128)}), f32[96,3,192]{2,0,1:T(8,128)}) %reduce-scatter.9.cloned.1.call-update) | async-done | bytes 221200 | tf_op jit(solution)/shard_map/reduce_scatter | solution.py:179
  (192 shorter events, 34.1 us)
Async XLA Ops:
  7.2 145.7 %copy-start = (bf16[768,768]{1,0:T(8,128)(2,1)S(1)}, bf16[768,768]{1,0:T(8,128)(2,1)}, u32[]{:S(2)}) copy-start(bf16[768,768]{1,0:T(8,128)(2,1)} %param.29) | copy-start | bytes 3538948
  7.2 9.3 %copy-start.4 = (bf16[1536,768]{1,0:T(8,128)(2,1)S(1)}, bf16[1536,768]{1,0:T(8,128)(2,1)}, u32[]{:S(2)}) copy-start(bf16[1536,768]{1,0:T(8,128)(2,1)} %param.19) | copy-start | bytes 7077892
  7.2 140.2 %all-reduce.14.cloned.1.call-start = ((), (), s32[]{:S(2)}) async-start(), calls=%async_computation.4 | async-start | bytes 9437184 | tf_op jit(solution)/shard_map/psum | solution.py:114
  8.1 10.2 %copy-start.25 = (f32[768]{0:T(1024)}, f32[768]{0:T(1024)S(1)}, u32[]{:S(2)}) copy-start(f32[768]{0:T(1024)S(1)} %convert_element_type.122) | copy-start | bytes 9220
  8.9 9.4 %copy-start.34 = (f32[768]{0:T(1024)}, f32[768]{0:T(1024)S(1)}, u32[]{:S(2)}) copy-start(f32[768]{0:T(1024)S(1)} %convert_element_type.123) | copy-start | bytes 9220
  11.6 4.8 copy-start.38
  11.6 4.8 copy-start.39
  11.6 4.8 copy-start.44
  13.8 4.5 copy-start.18
  16.3 2.0 copy-start.21
  43.9 6.5 copy-start.20
  45.7 0.8 copy-start.10
  50.4 0.7 copy-start.40
  50.5 1.3 copy-start.36
  50.5 1.9 copy-start.41
  50.5 218.2 %all-reduce.16.cloned.1.call-start = ((), (), s32[]{:S(2)}) async-start(), calls=%async_computation.5 | async-start | bytes 9437184 | tf_op jit(solution)/shard_map/psum | solution.py:145
  147.4 5.5 slice-start.2
  150.5 2.4 copy-start.2
  150.5 0.8 copy-start.23
  150.5 0.8 copy-start.30
  150.5 3.9 slice-start.3
  151.2 3.2 copy-start.37
  154.4 20.6 %copy-start.9 = (bf16[1536,768]{1,0:T(8,128)(2,1)}, bf16[1536,768]{1,0:T(8,128)(2,1)S(1)}, u32[]{:S(2)}) copy-start(bf16[1536,768]{1,0:T(8,128)(2,1)S(1)} %add_convert_fusion.1) | copy-start | bytes 7077892
  168.7 1.4 copy-start.12
  174.4 176.1 %reduce-scatter.15.cloned.1.call-start = ((), (), s32[]{:S(2)}) async-start(), calls=%async_computation.9 | async-start | bytes 884736
  175.0 14.5 %copy-start.43 = (bf16[768,768]{1,0:T(8,128)(2,1)S(1)}, bf16[768,768]{1,0:T(8,128)(2,1)}, u32[]{:S(2)}) copy-start(bf16[768,768]{1,0:T(8,128)(2,1)} %param.31) | copy-start | bytes 3538948
  187.9 1.5 copy-start.47
  189.4 79.3 %copy-start.24 = (f32[768]{0:T(1024)S(1)}, f32[768]{0:T(1024)}, u32[]{:S(2)}) copy-start(f32[768]{0:T(1024)} %convert_element_type.131) | copy-start | bytes 9220
  193.7 80.6 %copy-start.13 = (bf16[1536,768]{1,0:T(8,128)(2,1)S(1)}, bf16[1536,768]{1,0:T(8,128)(2,1)}, u32[]{:S(2)}) copy-start(bf16[1536,768]{1,0:T(8,128)(2,1)} %param.33) | copy-start | bytes 7077892
  268.7 5.6 copy-start.7
  274.3 7.1 copy-start.11
  279.3 2.2 copy-start.3
  279.3 4.1 copy-start.17
  283.4 4.2 copy-start.15
  286.8 235.0 %all-reduce.18.cloned.1.call-start = ((), (), s32[]{:S(2)}) async-start(), calls=%async_computation.10 | async-start | bytes 18874368 | tf_op jit(solution)/shard_map/psum | solution.py:123
  308.7 1.2 copy-start.16
  309.9 6.9 copy-start.45
  322.6 1.7 copy-start.14
  322.6 273.6 %reduce-scatter.13.cloned.1.call-start = ((), (), s32[]{:S(2)}) async-start(), calls=%async_computation.8 | async-start | bytes 2654208 | tf_op jit(solution)/shard_map/reduce_scatter | solution.py:185
  329.4 6.6 copy-start.5
  329.4 6.6 copy-start.19
  329.4 6.6 copy-start.22
  329.4 6.6 copy-start.26
  329.4 6.6 copy-start.35
  329.4 339.6 %reduce-scatter.11.cloned.1.call-start = ((), (), s32[]{:S(2)}) async-start(), calls=%async_computation.7 | async-start | bytes 2654208 | tf_op jit(solution)/shard_map/reduce_scatter | solution.py:187
  335.9 5.6 copy-start.46
  335.9 7.5 %copy-start.42 = (bf16[768]{0:T(1024)(128)(2,1)S(1)}, bf16[768]{0:T(1024)(128)(2,1)}, u32[]{:S(2)}) copy-start(bf16[768]{0:T(1024)(128)(2,1)} %param.32) | copy-start | bytes 4612
  335.9 7.5 %copy-start.33 = (f32[768]{0:T(1024)S(1)}, f32[768]{0:T(1024)}, u32[]{:S(2)}) copy-start(f32[768]{0:T(1024)} %get-tuple-element.191) | copy-start | bytes 9220
  335.9 406.1 %reduce-scatter.9.cloned.1.call-start = ((), (), s32[]{:S(2)}) async-start(), calls=%async_computation.6 | async-start | bytes 2654208 | tf_op jit(solution)/shard_map/reduce_scatter | solution.py:179
  341.5 184.7 %copy-start.28 = (f32[768]{0:T(1024)S(1)}, f32[768]{0:T(1024)}, u32[]{:S(2)}) copy-start(f32[768]{0:T(1024)} %get-tuple-element.138) | copy-start | bytes 9220
  341.5 184.7 %copy-start.29 = (f32[768]{0:T(1024)S(1)}, f32[768]{0:T(1024)}, u32[]{:S(2)}) copy-start(f32[768]{0:T(1024)} %get-tuple-element.144) | copy-start | bytes 9220
  341.5 184.7 %copy-start.31 = (f32[768]{0:T(1024)S(1)}, f32[768]{0:T(1024)}, u32[]{:S(2)}) copy-start(f32[768]{0:T(1024)} %get-tuple-element.182) | copy-start | bytes 9220
  341.5 184.7 %copy-start.32 = (f32[768]{0:T(1024)S(1)}, f32[768]{0:T(1024)}, u32[]{:S(2)}) copy-start(f32[768]{0:T(1024)} %get-tuple-element.190) | copy-start | bytes 9220
  521.8 53.2 %slice-start = ((s8[4718592]{0:T(1024)(128)(4,1)}), s8[524288]{0:T(1024)(128)(4,1)S(1)}, s32[]{:S(2)}) async-start(s8[4718592]{0:T(1024)(128)(4,1)} %bitcast.156), calls=%async_computation.11 | async-start | bytes 1048576
  568.9 6.1 slice-start.1
  568.9 6.1 copy-start.6
  568.9 8.0 %copy-start.8 = (f32[1536,768]{1,0:T(8,128)S(1)}, f32[1536,768]{1,0:T(8,128)}, u32[]{:S(2)}) copy-start(f32[1536,768]{1,0:T(8,128)} %get-tuple-element.181) | copy-start | bytes 14155780
  569.0 8.0 %copy-start.27 = (f32[768]{0:T(1024)S(1)}, f32[768]{0:T(1024)}, u32[]{:S(2)}) copy-start(f32[768]{0:T(1024)} %copy-done.25) | copy-start | bytes 9220
  569.0 173.0 %copy-start.1 = (bf16[768,768]{1,0:T(8,128)(2,1)S(1)}, bf16[768,768]{1,0:T(8,128)(2,1)}, u32[]{:S(2)}) copy-start(bf16[768,768]{1,0:T(8,128)(2,1)} %param.29) | copy-start | bytes 3538948
Sparse Core Ops, SparseCore 0:
  50.6 96.7 all-reduce.13
  174.5 94.1 all-reduce.15
  286.9 63.5 reduce-scatter.14
  352.9 168.8 all-reduce.17
  525.7 70.4 reduce-scatter.12
  600.1 68.9 reduce-scatter.10
  673.1 68.8 reduce-scatter.8
where the time goes:
time: 756 us; the launch traced here: 749 us
  waiting for transfers between devices  500 us (66%)
  matrix products  93.4 us (12%)
  local copies, waits for them, and re-layouts  51.9 us (7%)
  other arithmetic  48.3 us (6%)
  blocking collectives  37.9 us (5%)
  between operations  16.3 us (2%)
    psum x1, waiting for transfers between devices, shards(): fed = lax.psum(column_part, 'mp')  170 us
    psum x1, waiting for transfers between devices, shards(): attended = lax.psum(head_part, 'mp')  87.3 us
    psum x1, waiting for transfers between devices, shards(): grad_normed2 = lax.psum(column_back_part, 'mp')  75 us
    reduce_scatter x1, waiting for transfers between devices, shards(): lax.psum_scatter(qkv_weight_grad, 'dp', scatter_dimension=0, tiled=True)  72.9 us
    reduce_scatter x1, waiting for transfers between devices, shards(): lax.psum_scatter(up_weight_grad, 'dp', scatter_dimension=0, tiled=True)  72.9 us
    unnamed x1, blocking collectives  37.9 us
    unnamed x117, local copies, waits for them, and re-layouts  20.4 us
    reduce_scatter x1, waiting for transfers between devices, shards(): lax.psum_scatter(down_weight_grad, 'dp', scatter_dimension=1, tiled=True)  16.4 us
  transfers between devices with their start and end apart: 7, of which 7 were waited for; matrix products, arithmetic and copies ran while one was open for 13% of the time, Pallas kernels for 0%

commit v1 on v0

--- a/solution.py
+++ b/solution.py
@@ -120,7 +120,11 @@
     activated, gelu_pull = jax.vjp(exact_gelu, hidden_pre)
     hidden = activated.astype(jnp.bfloat16)
     column_part = jnp.dot(hidden, down_weight, preferred_element_type=jnp.float32)
-    fed = lax.psum(column_part, "mp")
+
+    def change_loops(local, ax_name):
+        return jnp.sum(lax.all_gather(local, axis_name=ax_name), axis=0)
+
+    fed = change_loops(column_part, "mp")
     layer_output = (middle + fed + down_bias.astype(jnp.float32)).astype(jnp.bfloat16)
     grad_out = cotangent.astype(jnp.float32)
     down_bias_grad = jnp.sum(grad_out, axis=0)

time: 756 us -> 810 us (1.071)
  waiting for transfers between devices: 500 us -> 544 us
  other arithmetic: 48.3 us -> 59.6 us
    all_gather x0 -> x1, waiting for transfers between devices: none -> 116 us  [change_loops(): return jnp.sum(lax.all_gather(local, axis_name=ax_name), axis=0)]
    psum x1, waiting for transfers between devices: 170 us -> 93.6 us  [shards(): grad_normed1 = lax.psum(head_back_part, 'mp')]
    reduce_sum x0 -> x1, other arithmetic: none -> 10.5 us  [change_loops(): return jnp.sum(lax.all_gather(local, axis_name=ax_name), axis=0)]
    unnamed x117 -> x105, local copies, waits for them, and re-layouts: 20.4 us -> 18.5 us
  transfers between devices with their start and end apart: 7 -> 8, of which waited for: 7 -> 8; matrix products, arithmetic and copies ran while one was open for 13% -> 13% of each run, Pallas kernels for 0% -> 0%
where the time goes in v1:
time: 810 us; the launch traced here: 803 us
  waiting for transfers between devices  544 us (67%)
  matrix products  93.4 us (12%)
  other arithmetic  59.6 us (7%)
  local copies, waits for them, and re-layouts  49.9 us (6%)
  blocking collectives  38.1 us (5%)
  between operations  16.2 us (2%)
    all_gather x1, waiting for transfers between devices, change_loops(): return jnp.sum(lax.all_gather(local, axis_name=ax_name), axis=0)  116 us
    psum x1, waiting for transfers between devices, shards(): grad_normed1 = lax.psum(head_back_part, 'mp')  93.6 us
    psum x1, waiting for transfers between devices, shards(): attended = lax.psum(head_part, 'mp')  87.3 us
    psum x1, waiting for transfers between devices, shards(): grad_normed2 = lax.psum(column_back_part, 'mp')  75 us
    reduce_scatter x1, waiting for transfers between devices, shards(): lax.psum_scatter(qkv_weight_grad, 'dp', scatter_dimension=0, tiled=True)  73.1 us
    reduce_scatter x1, waiting for transfers between devices, shards(): lax.psum_scatter(up_weight_grad, 'dp', scatter_dimension=0, tiled=True)  72.8 us
    unnamed x1, blocking collectives  38.1 us
    reduce_scatter x1, waiting for transfers between devices, shards(): lax.psum_scatter(down_weight_grad, 'dp', scatter_dimension=1, tiled=True)  20.4 us
  transfers between devices with their start and end apart: 8, of which 8 were waited for; matrix products, arithmetic and copies ran while one was open for 13% of the time, Pallas kernels for 0%

profile of v1, /device:TPU:0, one launch (start us, length us, event | category | flops | bytes accessed | tf_op | source)
XLA Modules:
  0.0 802.9 jit_solution(756818185542359470)
XLA Ops:
  7.3 0.8 convert_element_type.122
  11.6 2.1 convert_reduce_fusion
  13.8 2.5 fusion.42
  16.5 1.8 fusion.71
  18.3 1.5 add_convert_fusion.2
  19.8 5.2 reshape.266
  24.9 3.4 copy.53
  28.3 15.6 %while.22 = (s32[]{:T(128)}, bf16[3,512,3,64]{1,3,2,0:T(8,128)(2,1)}, f32[3,3,512,1]{2,1,3,0:T(4,128)}, bf16[3,512,3,3,64]{1,4,3,2,0:T(8,128)(2,1)}, s32[3,512]{1,0:T(4,128)S(1)}, /*index=5*/s32[]{:T(128)}) while((s32[]{:T(128)}, bf16[3,512,3,64]{1,3,2,0:T(8,128)(2,1)}, f32[3,3,512,1]{2,1,3,0:T(4,128)}, bf16[3,512,3,3,64]{1,4,3,2,0:T(8,128)(2,1)}, ...), condition=%wide.region_5.6_spmd, body=%wide.region_2.5_spmd.sunk | while | flops 211122688 | bytes 12513373 | solution.py:111
  28.6 1.1 dynamic-slice_bitcast_fusion.6
  31.2 1.8 fusion.120
  33.8 1.1 dynamic-slice_bitcast_fusion.6
  36.4 1.8 fusion.120
  39.0 1.1 dynamic-slice_bitcast_fusion.6
  41.6 1.8 fusion.120
  43.9 1.6 copy.54
  46.5 4.0 fusion.76
  52.5 1.3 convert_element_type.132
  53.8 6.4 fusion.78
  60.2 87.3 %all-reduce.13.cloned.1.call-done = f32[1536,768]{1,0:T(8,128)} async-done(((f32[1536,768]{1,0:T(8,128)}), f32[1536,768]{1,0:T(8,128)}) %all-reduce.13.cloned.1.call-update) | async-done | bytes 4718608 | tf_op jit(solution)/shard_map/psum | solution.py:114
  147.5 3.1 fusion.74
  151.3 1.1 add_convert_fusion.1
  153.0 1.5 slice-done.1
  154.5 14.3 %convert_reduce_fusion.2 = (f32[768]{0:T(1024)}, bf16[1536,768]{1,0:T(8,128)(2,1)S(1)}) fusion(f32[1536,768]{1,0:T(8,128)S(1)} %bitcast.167, f32[768]{0:T(1024)S(1)} %copy-done.33, bf16[1536,768]{1,0:T(8,128)(2,1)S(1)} %add_convert_fusion.1, bf16[768,768]{1,0:T(8,128)(2,1)S(1)} %copy-done), kind=kOutput, calls=%fused_computation.78 | convolution fusion | flops 1900412160 | bytes 10622976 | tf_op jit(solution)/shard_map/dot_general | solution.py:138
  168.8 1.4 copy-done.11
  170.2 4.3 fusion.79
  174.6 12.9 %fusion.46 = bf16[1536,768]{1,0:T(8,128)(2,1)S(1)} fusion(bf16[1536,768]{1,0:T(8,128)(2,1)S(1)} %add_convert_fusion.1, bf16[768,768]{1,0:T(8,128)(2,1)S(1)} %copy-done, f32[768]{0:T(1024)} %reshape.274), kind=kOutput, calls=%fused_computation.72 | convolution fusion | flops 1889796096 | bytes 5901312 | tf_op jit(solution)/shard_map/dot_general | solution.py:119
  187.5 1.4 copy-done.43
  189.0 4.3 fusion.77
  193.9 75.0 %all-reduce.15.cloned.1.call-done = f32[1536,768]{1,0:T(8,128)} async-done(((f32[1536,768]{1,0:T(8,128)}), f32[1536,768]{1,0:T(8,128)}) %all-reduce.15.cloned.1.call-update) | async-done | bytes 4718608 | tf_op jit(solution)/shard_map/psum | solution.py:149
  268.8 5.4 multiply_reduce_fusion.1
  274.3 116.3 %all-gather.3.cloned.1.call-done = f32[6144,768]{1,0:T(8,128)} async-done(((f32[1536,768]{1,0:T(8,128)}), f32[6144,768]{1,0:T(8,128)}) %all-gather.3.cloned.1.call-update) | async-done | bytes 18874384 | tf_op jit(solution)/shard_map/all_gather | solution.py:125
  390.6 10.5 %reduce_sum.184 = f32[1536,768]{1,0:T(8,128)} reduce(f32[4,1536,768]{2,1,0:T(8,128)} %bitcast.157, f32[]{:T(128)} %constant.63.clone.1), dimensions={0}, to_apply=%region_9.10 | reduce | flops 3538944 | bytes 23592964 | tf_op jit(solution)/shard_map/reduce_sum | solution.py:125
  401.2 8.0 fusion.73
  409.2 2.1 copy-done.3
  411.3 1.9 convolution_bitcast_fusion.1
  413.2 3.4 convolution_convert_fusion
  417.5 21.1 %while.23 = (s32[]{:T(128)}, bf16[3,512,3,3,64]{1,4,3,2,0:T(8,128)(2,1)S(1)}, bf16[3,512,3,3,64]{1,4,3,2,0:T(8,128)(2,1)}, s32[3,512]{1,0:T(4,128)}, f32[3,3,512...) while((s32[]{:T(128)}, bf16[3,512,3,3,64]{1,4,3,2,0:T(8,128)(2,1)S(1)}, ...), condition=%wide.region_15.16_spmd, body=%wide.region_13.15_spmd.sunk | while | flops 512915968 | bytes 28481644 | solution.py:162
  419.1 1.1 dynamic-slice_bitcast_fusion.7
  420.9 1.1 multiply_reduce_fusion.7
  422.0 0.8 multiply_convert_fusion.2
  426.1 1.1 dynamic-slice_bitcast_fusion.7
  427.9 1.1 multiply_reduce_fusion.7
  429.0 0.8 multiply_convert_fusion.2
  433.2 1.1 dynamic-slice_bitcast_fusion.7
  434.9 1.1 multiply_reduce_fusion.7
  436.1 0.8 multiply_convert_fusion.2
  438.6 1.2 copy-done.13
  439.8 3.1 copy.57
  442.9 3.8 reshape.270
  446.6 5.8 convolution_bitcast_fusion
  452.5 1.6 copy-done.10
  454.1 5.1 fusion.81
  459.5 6.0 fusion.80
  465.7 5.4 fusion.66
  473.2 1.5 convert_reduce_fusion.4
  474.9 5.3 reduce-scatter.15.cloned.1.call-done
  480.2 1.6 copy.70
  481.8 93.6 %all-reduce.17.cloned.1.call-done = f32[1536,768]{1,0:T(8,128)} async-done(((f32[1536,768]{1,0:T(8,128)}), f32[1536,768]{1,0:T(8,128)}) %all-reduce.17.cloned.1.call-update) | async-done | bytes 4718608 | tf_op jit(solution)/shard_map/psum | solution.py:176
  575.4 4.6 fusion.41
  580.0 38.1 %all-reduce.8 = (f32[768]{0:T(1024)S(1)}, f32[768]{0:T(1024)S(1)}, f32[2,3,64]{2,1,0:T(4,128)S(1)}, f32[768]{0:T(1024)S(1)}, f32[768]{0:T(1024)S(1)}, /*index=5*...) all-reduce(f32[768]{0:T(1024)S(1)} %get-tuple-element.140, ...), channel_id=3, replica_groups=mesh['dp'=8,'mp'=4] {'dp'}, use_global_device_ids=true, to_apply=%region_20.21.clone | all-reduce | flops 5760 | bytes 46080
  623.8 5.7 fusion.40
  629.4 20.4 %reduce-scatter.13.cloned.1.call-done = f32[768,96]{0,1:T(8,128)} async-done(((f32[768,768]{0,1:T(8,128)}), f32[768,96]{0,1:T(8,128)}) %reduce-scatter.13.cloned.1.call-update) | async-done | bytes 294928 | tf_op jit(solution)/shard_map/reduce_scatter | solution.py:189
  649.9 72.8 %reduce-scatter.11.cloned.1.call-done = f32[96,768]{1,0:T(8,128)} async-done(((f32[768,768]{1,0:T(8,128)}), f32[96,768]{1,0:T(8,128)}) %reduce-scatter.11.cloned.1.call-update) | async-done | bytes 294928 | tf_op jit(solution)/shard_map/reduce_scatter | solution.py:191
  722.7 73.1 %reduce-scatter.9.cloned.1.call-done = f32[96,3,192]{2,0,1:T(8,128)} async-done(((f32[768,3,192]{2,0,1:T(8,128)}), f32[96,3,192]{2,0,1:T(8,128)}) %reduce-scatter.9.cloned.1.call-update) | async-done | bytes 221200 | tf_op jit(solution)/shard_map/reduce_scatter | solution.py:183
  (182 shorter events, 34.9 us)
Async XLA Ops:
  7.2 145.8 %copy-start = (bf16[768,768]{1,0:T(8,128)(2,1)S(1)}, bf16[768,768]{1,0:T(8,128)(2,1)}, u32[]{:S(2)}) copy-start(bf16[768,768]{1,0:T(8,128)(2,1)} %param.29) | copy-start | bytes 3538948
  7.2 9.3 %copy-start.4 = (bf16[1536,768]{1,0:T(8,128)(2,1)S(1)}, bf16[1536,768]{1,0:T(8,128)(2,1)}, u32[]{:S(2)}) copy-start(bf16[1536,768]{1,0:T(8,128)(2,1)} %param.19) | copy-start | bytes 7077892
  7.2 140.3 %all-reduce.13.cloned.1.call-start = ((), (), s32[]{:S(2)}) async-start(), calls=%async_computation.4 | async-start | bytes 9437184 | tf_op jit(solution)/shard_map/psum | solution.py:114
  8.1 10.2 %copy-start.22 = (f32[768]{0:T(1024)}, f32[768]{0:T(1024)S(1)}, u32[]{:S(2)}) copy-start(f32[768]{0:T(1024)S(1)} %convert_element_type.122) | copy-start | bytes 9220
  8.9 9.4 %copy-start.30 = (f32[768]{0:T(1024)}, f32[768]{0:T(1024)S(1)}, u32[]{:S(2)}) copy-start(f32[768]{0:T(1024)S(1)} %convert_element_type.123) | copy-start | bytes 9220
  11.6 4.8 copy-start.34
  11.6 4.8 copy-start.35
  11.6 4.8 copy-start.40
  13.8 4.5 copy-start.15
  16.3 2.0 copy-start.18
  43.9 6.6 copy-start.17
  45.7 0.8 copy-start.7
  50.5 0.7 copy-start.36
  50.5 1.3 copy-start.32
  50.5 1.9 copy-start.37
  50.6 218.3 %all-reduce.15.cloned.1.call-start = ((), (), s32[]{:S(2)}) async-start(), calls=%async_computation.5 | async-start | bytes 9437184 | tf_op jit(solution)/shard_map/psum | solution.py:149
  147.5 5.5 slice-start
  150.5 2.4 copy-start.2
  150.6 0.8 copy-start.20
  150.6 0.8 copy-start.28
  150.6 3.9 slice-start.1
  151.3 3.2 copy-start.33
  154.5 20.1 %copy-start.6 = (bf16[1536,768]{1,0:T(8,128)(2,1)}, bf16[1536,768]{1,0:T(8,128)(2,1)S(1)}, u32[]{:S(2)}) copy-start(bf16[1536,768]{1,0:T(8,128)(2,1)S(1)} %add_convert_fusion.1) | copy-start | bytes 7077892
  168.8 1.4 copy-start.11
  174.5 216.1 %all-gather.3.cloned.1.call-start = ((), (), s32[]{:S(2)}) async-start(), calls=%async_computation.10 | async-start | bytes 23592960 | tf_op jit(solution)/shard_map/all_gather | solution.py:125
  174.6 14.4 %copy-start.39 = (bf16[768,768]{1,0:T(8,128)(2,1)S(1)}, bf16[768,768]{1,0:T(8,128)(2,1)}, u32[]{:S(2)}) copy-start(bf16[768,768]{1,0:T(8,128)(2,1)} %param.31) | copy-start | bytes 3538948
  187.5 1.5 copy-start.43
  193.2 0.7 copy-start.38
  193.2 75.6 %copy-start.21 = (f32[768]{0:T(1024)S(1)}, f32[768]{0:T(1024)}, u32[]{:S(2)}) copy-start(f32[768]{0:T(1024)} %convert_element_type.131) | copy-start | bytes 9220
  193.2 287.0 %reduce-scatter.15.cloned.1.call-start = ((), (), s32[]{:S(2)}) async-start(), calls=%async_computation.11 | async-start | bytes 884736
  390.6 10.5 %copy-start.9 = (bf16[1536,768]{1,0:T(8,128)(2,1)S(1)}, bf16[1536,768]{1,0:T(8,128)(2,1)}, u32[]{:S(2)}) copy-start(bf16[1536,768]{1,0:T(8,128)(2,1)} %param.33) | copy-start | bytes 7077892
  401.1 10.1 %copy-start.8 = (bf16[24,8,3,512]{3,1,2,0:T(8,128)(2,1)S(1)}, bf16[24,8,3,512]{3,1,2,0:T(8,128)(2,1)}, u32[]{:S(2)}) copy-start(bf16[24,8,3,512]{3,1,2,0:T(8,128)(2,1)} %copy-done.7) | copy-start | bytes 1769476
  409.2 2.1 copy-start.3
  409.2 4.1 copy-start.14
  413.2 4.2 copy-start.12
  416.7 158.7 %all-reduce.17.cloned.1.call-start = ((), (), s32[]{:S(2)}) async-start(), calls=%async_computation.6 | async-start | bytes 9437184 | tf_op jit(solution)/shard_map/psum | solution.py:176
  438.6 1.2 copy-start.13
  439.8 6.8 copy-start.41
  452.4 1.7 copy-start.10
  452.4 197.5 %reduce-scatter.13.cloned.1.call-start = ((), (), s32[]{:S(2)}) async-start(), calls=%async_computation.9 | async-start | bytes 2654208 | tf_op jit(solution)/shard_map/reduce_scatter | solution.py:189
  459.2 6.4 copy-start.5
  459.2 6.4 copy-start.16
  459.2 6.4 copy-start.19
  459.3 6.4 copy-start.23
  459.3 6.4 copy-start.31
  459.3 263.4 %reduce-scatter.11.cloned.1.call-start = ((), (), s32[]{:S(2)}) async-start(), calls=%async_computation.8 | async-start | bytes 2654208 | tf_op jit(solution)/shard_map/reduce_scatter | solution.py:191
  465.6 5.6 copy-start.42
  465.6 7.5 copy-start.29
  465.6 330.2 %reduce-scatter.9.cloned.1.call-start = ((), (), s32[]{:S(2)}) async-start(), calls=%async_computation.7 | async-start | bytes 2654208 | tf_op jit(solution)/shard_map/reduce_scatter | solution.py:183
  471.2 108.8 %copy-start.24 = (f32[768]{0:T(1024)S(1)}, f32[768]{0:T(1024)}, u32[]{:S(2)}) copy-start(f32[768]{0:T(1024)} %get-tuple-element.138) | copy-start | bytes 9220
  471.2 108.8 %copy-start.25 = (f32[768]{0:T(1024)S(1)}, f32[768]{0:T(1024)}, u32[]{:S(2)}) copy-start(f32[768]{0:T(1024)} %get-tuple-element.144) | copy-start | bytes 9220
  471.2 108.8 %copy-start.26 = (f32[768]{0:T(1024)S(1)}, f32[768]{0:T(1024)}, u32[]{:S(2)}) copy-start(f32[768]{0:T(1024)} %get-tuple-element.180) | copy-start | bytes 9220
  471.2 108.7 %copy-start.27 = (f32[768]{0:T(1024)S(1)}, f32[768]{0:T(1024)}, u32[]{:S(2)}) copy-start(f32[768]{0:T(1024)} %get-tuple-element.189) | copy-start | bytes 9220
  623.0 172.8 %copy-start.1 = (bf16[768,768]{1,0:T(8,128)(2,1)S(1)}, bf16[768,768]{1,0:T(8,128)(2,1)}, u32[]{:S(2)}) copy-start(bf16[768,768]{1,0:T(8,128)(2,1)} %param.29) | copy-start | bytes 3538948
Sparse Core Ops, SparseCore 0:
  50.7 96.7 all-reduce.12
  174.6 94.1 all-reduce.14
  270.4 120.1 all-gather.2
  416.8 63.3 reduce-scatter.14
  482.4 92.9 all-reduce.16
  579.3 70.5 reduce-scatter.12
  653.9 68.6 reduce-scatter.10
  726.7 69.0 reduce-scatter.8
